TPU v7x, 256 devices: a whole 4x4x8 slice. The times are simulated.
256 devices in a mesh: replica: 16 (over z, core), model: 4 (over x), copy: 4 (over y).
Axes of the slice: x: 4, y: 4, z: 8, core: 2. Of those that a mesh axis runs over, the one named last changes fastest.
Arguments:
- slope_up: bfloat16 [64, 1280, 5120], P(('copy', 'replica'), None, 'model'), parts along dimension 0, may hold values from -0.875 to 0.875
- slope_down: bfloat16 [64, 5120, 1280], P(('copy', 'replica'), 'model'), parts along dimension 0, may hold values from -0.875 to 0.875
- slope_norm: bfloat16 [64, 1280], P(('copy', 'replica')), parts along dimension 0, may hold values from -8 to 8
- param_up: float32 [5120, 5120], P(('copy', 'replica'), 'model'), parts along dimension 0, may hold values from -0.25 to 0.25
- param_down: float32 [20480, 1280], P(('copy', 'model'), 'replica'), parts along dimension 0, may hold values from -0.125 to 0.125
- param_norm: float32 [5120], P(('copy', 'replica')), parts along dimension 0, may hold values from 0.25 to 1.75
Outputs:
- half_up: bfloat16 [5120, 5120], P('copy', 'model'), parts along dimension 0
- half_down: bfloat16 [20480, 1280], P(('copy', 'model')), parts along dimension 0
- half_norm: bfloat16 [5120], P('copy'), parts along dimension 0
- next_up: float32 [5120, 5120], P(('copy', 'replica'), 'model'), parts along dimension 0
- next_down: float32 [20480, 1280], P(('copy', 'model'), 'replica'), parts along dimension 0
- next_norm: float32 [5120], P(('copy', 'replica')), parts along dimension 0
There are 4 independent parts, one for each index of `copy`. A program takes and returns all parts, laid end to end along the dimension named above; each array names one. Nothing has to cross between parts.
All inputs are finite; a program needn't handle non-finite values.
Results may differ from a plain program's by a relative error of at most 0.011.
Values may be sent and summed in bfloat16 or wider, within the bound.
A program may use at most 128 MiB of HBM per device.

v0:
```python
import jax
import jax.numpy as jnp
from jax import lax
from jax.sharding import PartitionSpec as P

learn_rate = 0.5


def cut_along(x, dim, count):
    dims = x.shape
    pieces = x.reshape(*dims[:dim], count, dims[dim] // count, *dims[dim + 1 :])
    return jnp.moveaxis(pieces, dim, 0)


def sum_together(arrays, axis, dims):
    count = lax.axis_size(axis)
    pieces = [cut_along(a, dim, count) for a, dim in zip(arrays, dims)]
    lines = jnp.concatenate([b.reshape(count, -1) for b in pieces], axis=1)
    extent = max(16, -(-lines.shape[1] // 1024) * 8)
    lines = jnp.pad(lines, ((0, 0), (0, extent * 128 - lines.shape[1]))).reshape(-1, 128)
    vector, at, outs = (lax.psum_scatter(lines, axis, tiled=True).reshape(-1), 0, [])
    for b in pieces:
        part = b[0]
        outs.append(vector[at : at + part.size].reshape(part.shape))
        at += part.size
    return tuple(outs)


def over_pieces(x, axis):
    return lax.all_gather(x, axis).sum(0)


def sent_to_all(x, axis):
    count = lax.axis_size(axis)
    return lax.all_to_all(jnp.broadcast_to(x[None], (count, *x.shape)), axis, 0, 0, tiled=True)


def taken_together(x, axis):
    return sent_to_all(x, axis).sum(axis=0)


def packed_total(arrays, axis):
    vector, at, outs = (jnp.concatenate([a.reshape(-1) for a in arrays]), 0, [])
    so_far = taken_together(vector, axis)
    for a in arrays:
        outs.append(so_far[at : at + a.size].reshape(a.shape))
        at += a.size
    return tuple(outs)


def turned_gather(arrays, axis, dims):
    turned = [jnp.moveaxis(a, dim, 0) for a, dim in zip(arrays, dims)]
    both = jnp.concatenate([t.reshape(len(t), -1) for t in turned], axis=1)
    out, at, outs = (lax.all_gather(both, axis, axis=0, tiled=True), 0, [])
    for t, dim in zip(turned, dims):
        piece = out[:, at : at + t[0].size].reshape(-1, *t.shape[1:])
        outs.append(jnp.moveaxis(piece, 0, dim))
        at += t[0].size
    return tuple(outs)


def shards(slope_up, slope_down, slope_norm, param_up, param_down, param_norm):
    mean_up, mean_down = tuple(
        (
            part.astype(jnp.float32)
            for part in sum_together(
                (
                    slope_up[0].astype(jnp.float32).astype(jnp.bfloat16),
                    slope_down[0].astype(jnp.float32).astype(jnp.bfloat16),
                ),
                "replica",
                (0, 1),
            )
        )
    )
    whole_norm = over_pieces(slope_norm[0].astype(jnp.float32), "replica")
    place = lax.axis_index("replica")
    mean_norm = lax.dynamic_slice_in_dim(
        whole_norm, place * param_norm.shape[0], param_norm.shape[0]
    )
    mean_rate = lax.axis_size("replica") ** (-0.5)
    mean_up = mean_up * mean_rate
    mean_down = mean_down * mean_rate
    mean_norm = mean_norm * mean_rate
    own_up, own_down, slope_up_norm, slope_down_norm = packed_total(
        (
            jnp.sum(param_up * param_up, axis=1, keepdims=True),
            jnp.sum(param_down * param_down, axis=0, keepdims=True),
            jnp.sum(mean_up * mean_up, axis=1, keepdims=True),
            jnp.sum(mean_down * mean_down, axis=0, keepdims=True),
        ),
        "model",
    )
    mean_up = mean_up * (jnp.sqrt(own_up) * lax.rsqrt(slope_up_norm + 1e-06))
    mean_down = mean_down * (jnp.sqrt(own_down) * lax.rsqrt(slope_down_norm + 1e-06))
    next_up = param_up - learn_rate * mean_up
    next_down = param_down - learn_rate * mean_down
    next_norm = param_norm - learn_rate * mean_norm
    half_up, half_down, half_norm = turned_gather(
        (
            next_up.astype(jnp.bfloat16),
            next_down.astype(jnp.bfloat16),
            next_norm.astype(jnp.bfloat16),
        ),
        "replica",
        (0, 1, 0),
    )
    return (half_up, half_down, half_norm, next_up, next_down, next_norm)


def solution(mesh):
    return jax.shard_map(
        shards,
        mesh=mesh,
        in_specs=(
            P(("copy", "replica"), None, "model"),
            P(("copy", "replica"), "model", None),
            P(("copy", "replica"), None),
            P(("copy", "replica"), "model"),
            P(("copy", "model"), "replica"),
            P(("copy", "replica")),
        ),
        out_specs=(
            P("copy", "model"),
            P(("copy", "model"), None),
            P("copy"),
            P(("copy", "replica"), "model"),
            P(("copy", "model"), "replica"),
            P(("copy", "replica")),
        ),
        check_vma=False,
    )
```

profile of v0, /device:TPU:1, one launch (start us, length us, event | category | flops | bytes accessed | tf_op | source)
XLA Modules:
  0.0 202.2 jit_solution(13785424861202217749)
XLA Ops:
  7.2 2.9 %reshape_reshape.3 = bf16[16,102400]{1,0:T(8,128)(2,1)S(1)} reshape(bf16[1,1280,1280]{2,1,0:T(8,128)(2,1)} %param.6) | data formatting | bytes 6553600 | tf_op jit(solution)/shard_map/reshape;reshape | solution.py:18
  10.2 5.7 %copy.36 = bf16[1,1280,1280]{1,2,0:T(8,128)(2,1)} copy(bf16[1,1280,1280]{2,1,0:T(8,128)(2,1)} %param.7) | data formatting | bytes 6553600 | tf_op args[1]
  15.8 7.3 %copy.37 = bf16[16,1280,80]{2,1,0:T(8,128)(2,1)} copy(bf16[16,1280,80]{1,2,0:T(8,128)(2,1)} %bitcast.12) | data formatting | bytes 6553600 | tf_op jit(solution)/shard_map/transpose | solution.py:12
  23.1 13.6 %reshape.62 = bf16[16,102400]{1,0:T(8,128)(2,1)} reshape(bf16[16,1280,80]{2,1,0:T(8,128)(2,1)} %copy.37) | data formatting | bytes 6553600 | tf_op jit(solution)/shard_map/reshape | solution.py:18
  36.7 8.6 %pad_maximum_fusion = bf16[16,204800]{1,0:T(8,128)(2,1)} fusion(bf16[16,102400]{1,0:T(8,128)(2,1)} %reshape.62, bf16[16,102400]{1,0:T(8,128)(2,1)S(1)} %reshape_reshape.3), kind=kLoop, calls=%fused_computation | loop fusion | flops 13107200 | bytes 13107200 | tf_op jit(solution)/shard_map/concatenate | solution.py:18
  45.3 6.6 %reshape.63 = bf16[25600,128]{1,0:T(8,128)(2,1)} reshape(bf16[16,204800]{1,0:T(8,128)(2,1)} %pad_maximum_fusion) | data formatting | bytes 13107200 | tf_op jit(solution)/shard_map/reshape | solution.py:20
  52.0 0.6 copy-done.2
  52.6 21.8 %all-gather = f32[16,1,1280]{2,1,0:T(1,128)S(1)} all-gather(f32[1,1,1280]{2,1,0:T(1,128)S(1)} %bitcast_convert_fusion), channel_id=1, replica_groups=mesh['replica'=16,'model'=4,'copy'=4] {'replica'}, dimensions={0}, use_global_device_ids=true | all-gather | bytes 87040 | tf_op jit(solution)/shard_map/all_gather | solution.py:30
  74.5 0.1 multiply_reduce_fusion.3
  74.6 0.1 multiply_reduce_fusion.2
  74.7 45.6 %reduce-scatter.2.cloned.1.call-done = bf16[1600,128]{1,0:T(8,128)(2,1)} async-done(((bf16[25600,128]{1,0:T(8,128)(2,1)}), bf16[1600,128]{1,0:T(8,128)(2,1)}) %reduce-scatter.2.cloned.1.call-update) | async-done | bytes 409616 | tf_op jit(solution)/shard_map/reduce_scatter | solution.py:21
  120.4 1.1 multiply_reduce_fusion.1
  121.5 0.1 reduce_sum.64
  121.6 0.1 reduce_sum.65
  121.8 1.1 slice_convert_fusion.1
  122.8 0.3 reshape.67
  123.2 0.2 multiply_reduce_fusion
  123.3 0.1 pad_maximum_fusion.2
  123.4 0.6 broadcast_in_dim.2
  124.0 4.0 %all-to-all-start = ((f32[4,1,320]{2,1,0:T(1,128)}), f32[4,1,320]{2,1,0:T(1,128)S(1)}, u32[]{:S(2)}, u32[]{:S(2)}) async-start(f32[4,1,320]{2,1,0:T(1,128)} %broadcast_in_dim.2), calls=%async_computation.1 | async-start | bytes 12288 | tf_op jit(solution)/shard_map/all_to_all | solution.py:35
  128.0 0.6 convert_bitcast_fusion.1
  128.6 0.1 copy.40
  128.7 0.2 copy.39
  129.0 3.1 %all-to-all-done = f32[4,1,320]{2,1,0:T(1,128)S(1)} async-done(((f32[4,1,320]{2,1,0:T(1,128)}), f32[4,1,320]{2,1,0:T(1,128)S(1)}, u32[]{:S(2)}, u32[]{:S(2)}) %all-to-all-start) | async-done | bytes 5152 | tf_op jit(solution)/shard_map/all_to_all | solution.py:35
  132.2 0.1 multiply_multiply_fusion.1
  132.3 0.9 fusion
  133.2 0.9 convert_bitcast_fusion
  134.0 0.8 pad_maximum_fusion.1
  134.8 50.4 %all-gather.3.cloned.1.call-done = bf16[1280,2561]{1,0:T(8,128)(2,1)} async-done(((bf16[80,2561]{1,0:T(8,128)(2,1)}), bf16[1280,2561]{1,0:T(8,128)(2,1)}) %all-gather.3.cloned.1.call-update) | async-done | bytes 6556176 | tf_op jit(solution)/shard_map/all_gather | solution.py:54
  185.2 5.1 %slice_bitcast_fusion = (bf16[1280,1280]{0,1:T(8,128)(2,1)S(1)}, bf16[1280,1280]{1,0:T(8,128)(2,1)}) fusion(bf16[1280,2561]{1,0:T(8,128)(2,1)} %all-gather.3.cloned.1.call-done), kind=kLoop, calls=%fused_computation.1 | loop fusion | bytes 13107200 | tf_op jit(solution)/shard_map/transpose | solution.py:57
  190.3 3.4 %copy.41 = bf16[1280,1280]{1,0:T(8,128)(2,1)} copy(bf16[1280,1280]{0,1:T(8,128)(2,1)S(1)} %get-tuple-element.48) | data formatting | bytes 6553600
  193.6 1.7 slice_reduce_fusion
  (15 shorter events, 0.3 us)
Async XLA Ops:
  7.2 113.2 %reduce-scatter.2.cloned.1.call-start = ((), (), s32[]{:S(2)}) async-start(), calls=%async_computation.2 | async-start | bytes 6963200 | tf_op jit(solution)/shard_map/reduce_scatter | solution.py:21
  51.9 0.7 copy-start.2
  51.9 22.5 %copy-start = (f32[80,1280]{1,0:T(8,128)S(1)}, f32[80,1280]{1,0:T(8,128)}, u32[]{:S(2)}) copy-start(f32[80,1280]{1,0:T(8,128)} %param.9) | copy-start | bytes 1228804
  51.9 22.7 %copy-start.1 = (f32[1280,80]{0,1:T(8,128)S(1)}, f32[1280,80]{0,1:T(8,128)}, u32[]{:S(2)}) copy-start(f32[1280,80]{0,1:T(8,128)} %param.10) | copy-start | bytes 1228804
  51.9 76.1 %copy-start.3 = (f32[80]{0:T(128)S(1)}, f32[80]{0:T(128)}, u32[]{:S(2)}) copy-start(f32[80]{0:T(128)} %param.11) | copy-start | bytes 964
  124.0 8.1 %all-to-all-start = ((f32[4,1,320]{2,1,0:T(1,128)}), f32[4,1,320]{2,1,0:T(1,128)S(1)}, u32[]{:S(2)}, u32[]{:S(2)}) async-start(f32[4,1,320]{2,1,0:T(1,128)} %broadcast_in_dim.2), calls=%async_computation.1 | async-start | bytes 12288 | tf_op jit(solution)/shard_map/all_to_all | solution.py:35
  128.0 57.2 %all-gather.3.cloned.1.call-start = ((), (), s32[]{:S(2)}) async-start(), calls=%async_computation.3 | async-start | bytes 7311360 | tf_op jit(solution)/shard_map/all_gather | solution.py:54
Sparse Core Ops, SparseCore 0:
  52.1 68.2 reduce-scatter.1
  135.0 50.1 all-gather.2
where the time goes:
time: 203 us; the launch traced here: 202 us
  waiting for transfers between devices  99.2 us (49%)
  local copies, waits for them, and re-layouts  48.4 us (24%)
  blocking collectives  21.8 us (11%)
  other arithmetic  14.8 us (7%)
  between operations  14.1 us (7%)
  starting transfers between devices  4.03 us (2%)
    all_gather x1, waiting for transfers between devices, turned_gather(): out, at, outs = (lax.all_gather(both, axis, axis=0, tiled=True), 0, [])  50.4 us
    reduce_scatter x1, waiting for transfers between devices, sum_together(): lax.psum_scatter(lines, axis, tiled=True).reshape(-1)  45.6 us
    all_gather x1, blocking collectives, over_pieces(): return lax.all_gather(x, axis).sum(0)  21.8 us
    reshape x1, local copies, waits for them, and re-layouts, sum_together(): lines = jnp.concatenate([b.reshape(count, -1) for b in pieces], axis=1)  13.6 us
    unnamed x10, local copies, waits for them, and re-layouts  9.69 us
    concatenate x1, other arithmetic, sum_together(): lines = jnp.concatenate([b.reshape(count, -1) for b in pieces], axis=1)  8.61 us
    transpose x1, local copies, waits for them, and re-layouts, cut_along(): return jnp.moveaxis(pieces, dim, 0)  7.28 us
    reshape x1, local copies, waits for them, and re-layouts, sum_together(): jnp.pad(lines, ((0, 0), (0, extent * 128 - lines.shape[1])))  6.61 us
  transfers between devices with their start and end apart: 3, of which 3 were waited for; matrix products, arithmetic and copies ran while one was open for 1% of the time, Pallas kernels for 0%

commit v1 on v0

v1 whole, which is shorter than its diff:
```python
import functools

import jax
import jax.numpy as jnp
from jax import lax
from jax.experimental import pallas as pl
from jax.experimental.pallas import tpu as pltpu
from jax.sharding import PartitionSpec as P

learn_rate = 0.5
eps = 1e-06
MESH = pl.DeviceIdType.MESH
UP, DOWN = 0, 1


def kernel(
    size,
    chips,
    models,
    up_hbm,
    down_hbm,
    row_in,
    param_up_hbm,
    param_down_hbm,
    half_up,
    half_down,
    next_up,
    next_down,
    half_norm,
    next_norm,
    own_up,
    raw_down,
    own_down,
    pair_in,
    send_buf,
    recv_buf,
    gathered,
    param,
    mean,
    sizes,
    sizes_in,
    rows,
    load_sem,
    pair_send,
    pair_recv,
    rs_send,
    rs_recv,
    ag_send,
    ag_recv,
    fwd_send,
    fwd_recv,
    size_send,
    size_recv,
    row_send,
    row_recv,
):
    f32, bf16 = jnp.float32, jnp.bfloat16
    share = size // (2 * chips)
    cols = size // 2
    replica = lax.axis_index("replica")
    model = lax.axis_index("model")
    z, c = replica // 2, replica % 2
    partner = {"replica": z * 2 + (1 - c)}
    rate = (2 * chips) ** (-0.5)

    def chip_at(offset):
        return lax.rem(z + offset + 2 * chips, chips)

    def neighbour(d):
        return {"replica": chip_at(1 if d == 0 else -1) * 2 + c}

    def rows_of(chip, core):
        return pl.ds(pl.multiple_of((chip * 2 + core) * share, 16), share)

    def half_cols(h):
        return pl.ds(h * cols, cols)

    def rdma(src, dst, send, recv, device):
        return pltpu.make_async_remote_copy(
            src_ref=src, dst_ref=dst, send_sem=send, recv_sem=recv, device_id=device, device_id_type=MESH
        )

    pending = []
    own = (own_up, own_down)
    full = (half_up, gathered)
    order = (4, 3, -3, 2, -2, 1, -1, 0)

    up_loads = {}
    for i, o in enumerate(order):
        at = rows_of(chip_at(o), c)
        up_loads[o] = pltpu.make_async_copy(up_hbm.at[at, :], own_up.at[at, :], load_sem.at[i])
        up_loads[o].start()
    down_load = pltpu.make_async_copy(down_hbm, raw_down, load_sem.at[8])
    down_load.start()
    param_loads = [
        pltpu.make_async_copy(param_up_hbm, param.at[UP], load_sem.at[9]),
        pltpu.make_async_copy(param_down_hbm, param.at[DOWN], load_sem.at[10]),
    ]
    for load in param_loads:
        load.start()

    barrier = pltpu.get_barrier_semaphore()
    others = [partner, neighbour(0), neighbour(1)]
    others += [{"model": lax.rem(model + d, models)} for d in range(1, models)]
    for device in others:
        pl.semaphore_signal(barrier, inc=1, device_id=device, device_id_type=MESH)
    pl.semaphore_wait(barrier, len(others))

    def pair_copy(p, o, core):
        at = rows_of(chip_at(o), core)
        src = up_hbm if p == UP else own_down
        i = order.index(o)
        return rdma(src.at[at, :], pair_in.at[p, o % chips], pair_send.at[p, i], pair_recv.at[p, i], partner)

    def start_pairs(p):
        for o in order:
            copy = pair_copy(p, o, 1 - c)
            copy.start()
            pending.append(copy)

    ready = set()

    def pair_sum(p, o, h):
        if (p, o) not in ready:
            ready.add((p, o))
            if p == UP:
                up_loads[o].wait()
            pair_copy(p, o, c).wait_recv()
        mine = own[p][rows_of(chip_at(o), c), half_cols(h)]
        return mine.astype(f32) + pair_in[p, o % chips, :, half_cols(h)].astype(f32)

    def rs_index(d, k, h):
        return 0 if k == 0 else 2 * k - 1 + (h != d)

    def rs_copy(p, d, k, h):
        i = rs_index(d, k, h)
        return rdma(send_buf.at[p, d, i], recv_buf.at[p, d, i], rs_send.at[p, d, i], rs_recv.at[p, d, i], neighbour(d))

    def rs_step(p, k, long_half):
        for d in range(2):
            h = d if long_half else 1 - d
            value = pair_sum(p, (4 - k if d == 0 else k - 4) if k else 4, h)
            if k >= 2 or (k == 1 and long_half):
                rs_copy(p, d, k - 1, h).wait_recv()
                value = value + recv_buf[p, d, rs_index(d, k - 1, h)].astype(f32)
            send_buf[p, d, rs_index(d, k, h)] = value.astype(bf16)
            copy = rs_copy(p, d, k, h)
            copy.start()
            pending.append(copy)

    def size_copy(p, e):
        return rdma(
            sizes.at[p],
            sizes_in.at[p, e - 1],
            size_send.at[p, e - 1],
            size_recv.at[p, e - 1],
            {"model": lax.rem(model + e, models)},
        )

    def finish_sum(p):
        total = jnp.zeros((share, 1), f32)
        for h in range(2):
            for d in range(2):
                rs_copy(p, d, 3, h).wait_recv()
            value = pair_sum(p, 0, h)
            for d in range(2):
                value = value + recv_buf[p, d, rs_index(d, 3, h)].astype(f32)
            value = value * rate
            mean[p, :, half_cols(h)] = value
            total = total + jnp.sum(value * value, axis=1, keepdims=True)
        param_loads[p].wait()
        weights = jnp.sum(param[p] * param[p], axis=1, keepdims=True)
        lane = lax.broadcasted_iota(jnp.int32, (share, 128), 1)
        sizes[p] = jnp.where(lane < 64, total, weights)
        for e in range(1, models):
            copy = size_copy(p, e)
            copy.start()
            pending.append(copy)

    def update(p):
        both = sizes[p]
        for e in range(1, models):
            size_copy(p, e).wait_recv()
            both = both + sizes_in[p, e - 1]
        ratio = jnp.sqrt(both[:, 64:65]) * lax.rsqrt(both[:, 0:1] + eps)
        value = param[p] - learn_rate * (mean[p] * ratio)
        out = next_up if p == UP else next_down
        out[...] = value
        full[p][rows_of(z, c), :] = value.astype(bf16)
        copy = rdma(
            full[p].at[rows_of(z, c), :], full[p].at[rows_of(z, c), :], fwd_send.at[p, 14], fwd_recv.at[p, 14], partner
        )
        copy.start()
        pending.append(copy)

    def ag_index(d, k, h):
        return 2 * k + (h != d)

    def ag_copy(p, d, k, h, hop):
        chip = chip_at((-k - hop) if d == 0 else (k + hop))
        at = full[p].at[rows_of(chip, c), half_cols(h)]
        i = ag_index(d, k, h)
        return rdma(at, at, ag_send.at[p, d, i], ag_recv.at[p, d, i], neighbour(d))

    def forward_copy(p, d, k, h, core):
        chip = chip_at((-k - 1) if d == 0 else (k + 1))
        at = full[p].at[rows_of(chip, core), half_cols(h)]
        i = d * 7 + ag_index(d, k, h)
        return rdma(at, at, fwd_send.at[p, i], fwd_recv.at[p, i], partner)

    def ag_arrive(p, k, long_half):
        for d in range(2):
            h = d if long_half else 1 - d
            ag_copy(p, d, k, h, 1).wait_recv()
            copy = forward_copy(p, d, k, h, c)
            copy.start()
            pending.append(copy)

    def ag_step(p, k, long_half):
        for d in range(2):
            h = d if long_half else 1 - d
            if k:
                ag_copy(p, d, k - 1, h, 1).wait_recv()
            copy = ag_copy(p, d, k, h, 0)
            copy.start()
            pending.append(copy)
            if k:
                copy = forward_copy(p, d, k - 1, h, c)
                copy.start()
                pending.append(copy)

    def forwarded(p, k, long_half):
        for d in range(2):
            h = d if long_half else 1 - d
            forward_copy(p, d, k, h, 1 - c).wait_recv()

    def row_copy(d, k, hop):
        chip = chip_at((-k - hop) if d == 0 else (k + hop))
        at = rows.at[c, chip]
        return rdma(at, at, row_send.at[d, k], row_recv.at[d, k], neighbour(d))

    def row_step(k):
        for d in range(2):
            if k:
                if d == 1 and k == 4:
                    continue
                row_copy(d, k - 1, 1).wait_recv()
            if k < 4 - d:
                copy = row_copy(d, k, 0)
                copy.start()
                pending.append(copy)

    def row_pair(core):
        return rdma(rows.at[core], rows.at[core], row_send.at[0, 4], row_recv.at[0, 4], partner)

    def finish_rows():
        row_pair(1 - c).wait_recv()
        total = jnp.zeros((1, size), f32)
        gains = jnp.zeros((8, size), f32)
        wide = lax.broadcasted_iota(jnp.int32, (8, size), 1)
        for chip in range(chips):
            for core in range(2):
                total = total + rows[core, chip, :, :size]
                piece = jnp.broadcast_to(rows[core, chip, :, size:], (8, 128))
                piece = jnp.concatenate([piece] + [jnp.zeros((8, 128), f32)] * (size // 128 - 1), axis=1)
                start = (chip * 2 + core) * share
                moved = pltpu.roll(piece, start, 1) if start else piece
                gains = jnp.where((wide >= start) & (wide < start + share), moved, gains)
        gains = gains - learn_rate * (jnp.broadcast_to(total, (8, size)) * rate)
        half_norm[...] = gains[0:1].astype(bf16)
        shift = lax.rem(size - replica * share, size)
        next_norm[...] = pltpu.roll(gains, shift, 1)[0:1, 0:128]

    def turn_in(lo, hi):
        @pl.loop(lo, hi)
        def _(i):
            at = pl.ds(pl.multiple_of(i * 128, 128), 128)
            own_down[at, :] = raw_down[:, at].T

    low = (5 * chip_at(4)) // 4

    def turn_out(lo, hi):
        @pl.loop(lo, hi)
        def _(i):
            j = lax.rem(low + i, size // 128)
            at = pl.ds(pl.multiple_of(j * 128, 128), 128)
            half_down[:, at] = gathered[at, :].T

    L, S = True, False
    start_pairs(UP)
    rows[c, z] = row_in[...]
    rs_step(UP, 0, L)
    rs_step(UP, 1, S)
    row_step(0)
    down_load.wait()
    turn_in(0, size // 128)
    start_pairs(DOWN)
    rs_step(UP, 1, L)
    rs_step(UP, 2, S)
    row_step(1)
    rs_step(UP, 2, L)
    rs_step(UP, 3, S)
    row_step(2)
    rs_step(DOWN, 0, L)
    rs_step(UP, 3, L)
    rs_step(DOWN, 1, S)
    row_step(3)
    rs_step(DOWN, 1, L)
    finish_sum(UP)
    rs_step(DOWN, 2, S)
    rs_step(DOWN, 2, L)
    update(UP)
    rs_step(DOWN, 3, S)
    ag_step(UP, 0, L)
    rs_step(DOWN, 3, L)
    ag_step(UP, 0, S)
    row_step(4)
    copy = row_pair(c)
    copy.start()
    pending.append(copy)
    ag_step(UP, 1, L)
    finish_sum(DOWN)
    ag_step(UP, 1, S)
    ag_step(UP, 2, L)
    update(DOWN)
    ag_step(UP, 2, S)
    ag_step(DOWN, 0, L)
    ag_step(UP, 3, L)
    ag_step(DOWN, 0, S)
    ag_arrive(UP, 2, S)
    ag_step(DOWN, 1, L)
    ag_arrive(UP, 3, L)
    ag_step(DOWN, 1, S)
    finish_rows()
    ag_step(DOWN, 2, L)
    ag_step(DOWN, 2, S)
    rdma(
        full[DOWN].at[rows_of(z, 1 - c), :], full[DOWN].at[rows_of(z, 1 - c), :], fwd_send.at[DOWN, 14], fwd_recv.at[DOWN, 14], partner
    ).wait_recv()
    forwarded(DOWN, 0, L)
    forwarded(DOWN, 0, S)
    turn_out(5, 7)
    ag_step(DOWN, 3, L)
    forwarded(DOWN, 1, L)
    forwarded(DOWN, 1, S)
    turn_out(4, 5)
    turn_out(7, 8)
    ag_arrive(DOWN, 2, S)
    forwarded(DOWN, 2, L)
    forwarded(DOWN, 2, S)
    turn_out(2, 4)
    turn_out(8, 10)
    ag_arrive(DOWN, 3, L)
    rdma(
        full[UP].at[rows_of(z, 1 - c), :], full[UP].at[rows_of(z, 1 - c), :], fwd_send.at[UP, 14], fwd_recv.at[UP, 14], partner
    ).wait_recv()
    for k in range(3):
        forwarded(UP, k, L)
        forwarded(UP, k, S)
    forwarded(UP, 3, L)
    forwarded(DOWN, 3, L)
    turn_out(0, 2)
    for copy in pending:
        copy.wait_send()


def shards(chips, models, slope_up, slope_down, slope_norm, param_up, param_down, param_norm):
    size = slope_up.shape[-1]
    share = param_up.shape[0]
    row = jnp.concatenate(
        [slope_norm.astype(jnp.float32), jnp.pad(param_norm, (0, 128 - share))[None]], axis=1
    )
    f32, bf16 = jnp.float32, jnp.bfloat16
    any_space = pl.BlockSpec(memory_space=pl.ANY)
    vmem = pl.BlockSpec(memory_space=pltpu.VMEM)
    dma = pltpu.SemaphoreType.DMA
    half_up, half_down, next_up, next_down, half_norm, next_norm = pl.pallas_call(
        functools.partial(kernel, size, chips, models),
        name="summed_step",
        out_shape=(
            jax.ShapeDtypeStruct((size, size), bf16),
            jax.ShapeDtypeStruct((size, size), bf16),
            jax.ShapeDtypeStruct((share, size), f32),
            jax.ShapeDtypeStruct((share, size), f32),
            jax.ShapeDtypeStruct((1, size), bf16),
            jax.ShapeDtypeStruct((1, 128), f32),
        ),
        in_specs=[any_space, any_space, vmem, any_space, any_space],
        out_specs=[vmem] * 6,
        scratch_shapes=[
            pltpu.VMEM((size, size), bf16),
            pltpu.VMEM((size, size), bf16),
            pltpu.VMEM((size, size), bf16),
            pltpu.VMEM((2, chips, share, size), bf16),
            pltpu.VMEM((2, 2, 7, share, size // 2), bf16),
            pltpu.VMEM((2, 2, 7, share, size // 2), bf16),
            pltpu.VMEM((size, size), bf16),
            pltpu.VMEM((2, share, size), f32),
            pltpu.VMEM((2, share, size), f32),
            pltpu.VMEM((2, share, 128), f32),
            pltpu.VMEM((2, models - 1, share, 128), f32),
            pltpu.VMEM((2, chips, 1, size + 128), f32),
            dma((11,)),
            dma((2, 8)),
            dma((2, 8)),
            dma((2, 2, 7)),
            dma((2, 2, 7)),
            dma((2, 2, 7)),
            dma((2, 2, 7)),
            dma((2, 15)),
            dma((2, 15)),
            dma((2, models - 1)),
            dma((2, models - 1)),
            dma((2, 5)),
            dma((2, 5)),
        ],
        compiler_params=pltpu.CompilerParams(
            collective_id=0, has_side_effects=True, vmem_limit_bytes=40 * 1024 * 1024
        ),
    )(slope_up[0], slope_down[0], row, param_up, param_down.T)
    return (
        half_up,
        half_down,
        half_norm[0],
        next_up,
        next_down.T,
        next_norm[0, :share],
    )


def solution(mesh):
    chips = mesh.shape["replica"] // 2
    models = mesh.shape["model"]
    return jax.shard_map(
        functools.partial(shards, chips, models),
        mesh=mesh,
        in_specs=(
            P(("copy", "replica"), None, "model"),
            P(("copy", "replica"), "model", None),
            P(("copy", "replica"), None),
            P(("copy", "replica"), "model"),
            P(("copy", "model"), "replica"),
            P(("copy", "replica")),
        ),
        out_specs=(
            P("copy", "model"),
            P(("copy", "model"), None),
            P("copy"),
            P(("copy", "replica"), "model"),
            P(("copy", "model"), "replica"),
            P(("copy", "replica")),
        ),
        check_vma=False,
    )
```

time: 203 us -> 99 us (0.49)
  waiting for transfers between devices: 99.2 us -> 0 us
  Pallas kernels: 0 us -> 81.4 us
  local copies, waits for them, and re-layouts: 48.4 us -> 15.4 us
  blocking collectives: 21.8 us -> 0 us
  other arithmetic: 14.8 us -> 1.32 us
  between operations: 14.1 us -> 0.67 us
  starting transfers between devices: 4.03 us -> 0 us
    pallas_call x0 -> x1, Pallas kernels: none -> 81.4 us  [shards(): pl.pallas_call(functools.partial(kernel, size, chips, models), name='summ...]
    all_gather x1 -> x0, waiting for transfers between devices: 50.4 us -> none  [turned_gather(): out, at, outs = (lax.all_gather(both, axis, axis=0, tiled=True), 0, [])]
    reduce_scatter x1 -> x0, waiting for transfers between devices: 45.6 us -> none  [sum_together(): lax.psum_scatter(lines, axis, tiled=True).reshape(-1)]
    all_gather x1 -> x0, blocking collectives: 21.8 us -> none  [over_pieces(): return lax.all_gather(x, axis).sum(0)]
    reshape x3 -> x0, local copies, waits for them, and re-layouts: 20.3 us -> none  [the longest x1 13.6 us: sum_together(): lines = jnp.concatenate([b.reshape(count, -1) for b in pieces], axis=1)]
    transpose x2 -> x0, local copies, waits for them, and re-layouts: 12.3 us -> none  [the longest x1 7.28 us: cut_along(): return jnp.moveaxis(pieces, dim, 0)]
    concatenate x3 -> x1, other arithmetic: 9.47 us -> 0.01 us  [shards(): jnp.concatenate([slope_norm.astype(jnp.float32), jnp.pad(param_norm, (0,...]
    unnamed x10 -> x20, local copies, waits for them, and re-layouts: 9.69 us -> 14.2 us
  transfers between devices with their start and end apart: 3 -> 0, of which waited for: 3 -> 0; matrix products, arithmetic and copies ran while one was open for 1% -> 0% of each run, Pallas kernels for 0% -> 0%
where the time goes in v1:
time: 99 us; the launch traced here: 98.7 us
  Pallas kernels  81.4 us (82%)
  local copies, waits for them, and re-layouts  15.4 us (16%)
  other arithmetic  1.32 us (1%)
    pallas_call x1, Pallas kernels, shards(): pl.pallas_call(functools.partial(kernel, size, chips, models), name='summ...  81.4 us
    unnamed x20, local copies, waits for them, and re-layouts  14.2 us

profile of v1, /device:TPU:1, one launch (start us, length us, event | category | flops | bytes accessed | tf_op | source)
XLA Modules:
  0.0 98.7 jit_solution(14615338219848295630)
XLA Ops:
  0.6 0.7 pad_bitcast_fusion
  1.3 0.7 convert_element_type.5
  2.0 0.0 copy-start
  2.0 1.9 %copy-done = bf16[1,1280,1280]{2,1,0:T(8,128)(2,1)S(1)} copy-done((bf16[1,1280,1280]{2,1,0:T(8,128)(2,1)S(1)}, bf16[1,1280,1280]{2,1,0:T(8,128)(2,1)}, u32[]{:S(2)}) %copy-start) | copy-done | bytes 3276824
  3.9 0.0 copy-start.2
  3.9 1.0 %copy-done.2 = f32[80,1280]{1,0:T(8,128)S(1)} copy-done((f32[80,1280]{1,0:T(8,128)S(1)}, f32[80,1280]{1,0:T(8,128)}, u32[]{:S(2)}) %copy-start.2) | copy-done | bytes 409624
  4.9 0.0 copy-start.3
  4.9 1.0 %copy-done.3 = f32[1280,80]{0,1:T(8,128)S(1)} copy-done((f32[1280,80]{0,1:T(8,128)S(1)}, f32[1280,80]{0,1:T(8,128)}, u32[]{:S(2)}) %copy-start.3) | copy-done | bytes 409624
  5.9 81.4 %summed_step.1 = (bf16[1280,1280]{1,0:T(8,128)(2,1)S(1)}, bf16[1280,1280]{1,0:T(8,128)(2,1)S(1)}, f32[80,1280]{1,0:T(8,128)S(1)}, f32[80,1280]{1,0:T(8,128)S(1)}...) custom-call(bf16[1280,1280]{1,0:T(8,128)(2,1)S(1)} %bitcast.8, bf16[1280,1280]{1,0:T(8,128)(2,1)} %bitcast.11, ...), custom_call_target="tpu_custom_call" | custom-call | tf_op jit(solution)/shard_map/summed_step/pallas_call | solution.py:377
  87.3 0.0 copy-start.1
  87.3 1.7 %copy-done.1 = bf16[1280,1280]{1,0:T(8,128)(2,1)} copy-done((bf16[1280,1280]{1,0:T(8,128)(2,1)}, bf16[1280,1280]{1,0:T(8,128)(2,1)S(1)}, u32[]{:S(2)}) %copy-start.1) | copy-done | bytes 3276824
  89.0 0.0 copy-start.4
  89.0 0.8 copy-done.4
  89.8 0.0 copy-start.6
  89.8 0.7 copy-done.6
  90.5 0.5 slice_bitcast_fusion
  91.0 0.6 reduce
  91.7 3.8 %copy.16 = bf16[1280,1280]{1,0:T(8,128)(2,1)} copy(bf16[1280,1280]{1,0:T(8,128)(2,1)} %copy-done.1) | data formatting | bytes 6553600
  95.5 0.0 copy-start.7
  95.5 0.0 copy-start.5
  95.5 1.7 %copy.17 = bf16[1280,1280]{1,0:T(8,128)(2,1)} copy(bf16[1280,1280]{1,0:T(8,128)(2,1)S(1)} %get-tuple-element.25) | data formatting | bytes 6553600
  97.2 0.0 copy-done.7
  97.2 0.8 copy.18
  98.0 0.0 copy-done.5
  98.0 0.8 copy.19
  (1 shorter events, 0.0 us)
Async XLA Ops:
  2.0 1.9 %copy-start = (bf16[1,1280,1280]{2,1,0:T(8,128)(2,1)S(1)}, bf16[1,1280,1280]{2,1,0:T(8,128)(2,1)}, u32[]{:S(2)}) copy-start(bf16[1,1280,1280]{2,1,0:T(8,128)(2,1)} %param.6) | copy-start | bytes 9830404
  3.9 1.0 %copy-start.2 = (f32[80,1280]{1,0:T(8,128)S(1)}, f32[80,1280]{1,0:T(8,128)}, u32[]{:S(2)}) copy-start(f32[80,1280]{1,0:T(8,128)} %param_up_hbm.1) | copy-start | bytes 1228804
  4.9 1.0 %copy-start.3 = (f32[1280,80]{0,1:T(8,128)S(1)}, f32[1280,80]{0,1:T(8,128)}, u32[]{:S(2)}) copy-start(f32[1280,80]{0,1:T(8,128)} %param.10) | copy-start | bytes 1228804
  87.3 1.7 %copy-start.1 = (bf16[1280,1280]{1,0:T(8,128)(2,1)}, bf16[1280,1280]{1,0:T(8,128)(2,1)S(1)}, u32[]{:S(2)}) copy-start(bf16[1280,1280]{1,0:T(8,128)(2,1)S(1)} %get-tuple-element.24) | copy-start | bytes 9830404
  89.0 0.8 copy-start.4
  89.8 0.8 copy-start.6
  95.5 1.7 %copy-start.7 = (f32[80,1280]{1,0:T(8,128)S(1)}, f32[80,1280]{1,0:T(8,128)}, u32[]{:S(2)}) copy-start(f32[80,1280]{1,0:T(8,128)} %copy-done.6) | copy-start | bytes 1228804
  95.5 2.5 %copy-start.5 = (f32[80,1280]{1,0:T(8,128)S(1)}, f32[80,1280]{1,0:T(8,128)}, u32[]{:S(2)}) copy-start(f32[80,1280]{1,0:T(8,128)} %copy-done.4) | copy-start | bytes 1228804

commit v2 on v1

v2 whole, which is shorter than its diff:
```python
import functools

import jax
import jax.numpy as jnp
from jax import lax
from jax.experimental import pallas as pl
from jax.experimental.pallas import tpu as pltpu
from jax.sharding import PartitionSpec as P

learn_rate = 0.5
eps = 1e-06
MESH = pl.DeviceIdType.MESH
UP, DOWN = 0, 1


def kernel(
    size,
    chips,
    models,
    up_hbm,
    down_hbm,
    norm_hbm,
    param_up_hbm,
    param_down_hbm,
    gain_hbm,
    half_up,
    half_down,
    next_up,
    next_down,
    half_norm,
    next_norm,
    own_up,
    raw_down,
    own_down,
    pair_in,
    send_buf,
    recv_buf,
    gathered,
    param,
    mean,
    sizes,
    sizes_in,
    rows,
    norm_in,
    gain_in,
    load_sem,
    pair_send,
    pair_recv,
    rs_send,
    rs_recv,
    ag_send,
    ag_recv,
    fwd_send,
    fwd_recv,
    size_send,
    size_recv,
    row_send,
    row_recv,
):
    f32, bf16 = jnp.float32, jnp.bfloat16
    share = size // (2 * chips)
    cols = size // 2
    replica = lax.axis_index("replica")
    model = lax.axis_index("model")
    z, c = replica // 2, replica % 2
    partner = {"replica": z * 2 + (1 - c)}
    rate = (2 * chips) ** (-0.5)

    def chip_at(offset):
        return lax.rem(z + offset + 2 * chips, chips)

    def neighbour(d):
        return {"replica": chip_at(1 if d == 0 else -1) * 2 + c}

    def rows_of(chip, core):
        return pl.ds(pl.multiple_of((chip * 2 + core) * share, 16), share)

    def half_cols(h):
        return pl.ds(h * cols, cols)

    def rdma(src, dst, send, recv, device):
        return pltpu.make_async_remote_copy(
            src_ref=src, dst_ref=dst, send_sem=send, recv_sem=recv, device_id=device, device_id_type=MESH
        )

    own = (own_up, own_down)
    full = (half_up, gathered)
    order = (4, 3, -3, 2, -2, 1, -1, 0)

    def chip_rows(chip):
        return pl.ds(pl.multiple_of(chip * 2 * share, 32), 2 * share)

    def wait_bytes(ref, sem):
        pltpu.make_async_copy(ref, ref, sem).wait()

    def group(o):
        return 4 - abs(o)

    up_loads = {}
    for o in order:
        at = chip_rows(chip_at(o))
        sem = load_sem.at[max(group(o) - 1, 0)]
        up_loads[o] = pltpu.make_async_copy(up_hbm.at[at, :], own_up.at[at, :], sem)
    down_load = pltpu.make_async_copy(down_hbm, raw_down, load_sem.at[4])
    param_loads = [
        pltpu.make_async_copy(param_up_hbm, param.at[UP], load_sem.at[5]),
        pltpu.make_async_copy(param_down_hbm, param.at[DOWN], load_sem.at[6]),
    ]
    row_loads = [
        pltpu.make_async_copy(norm_hbm, norm_in, load_sem.at[7]),
        pltpu.make_async_copy(gain_hbm, gain_in, load_sem.at[8]),
    ]
    for o in order[:3]:
        up_loads[o].start()

    barrier = pltpu.get_barrier_semaphore()
    others = [partner, neighbour(0), neighbour(1)]
    others += [{"model": lax.rem(model + d, models)} for d in range(1, models)]
    for device in others:
        pl.semaphore_signal(barrier, inc=1, device_id=device, device_id_type=MESH)
    wait_bytes(own_up.at[0 : 6 * share, :], load_sem.at[0])
    for load in [down_load] + row_loads + [up_loads[o] for o in order[3:]] + param_loads:
        load.start()
    pl.semaphore_wait(barrier, len(others))

    def start_pairs(p, *offsets):
        for o in offsets:
            if p == UP and o in (2, 1, 0):
                wait_bytes(own_up.at[0 : (4 if o else 2) * share, :], load_sem.at[group(o) - 1])
            src = own[p].at[rows_of(chip_at(o), 1 - c), :]
            rdma(src, pair_in.at[p, o % chips], pair_send.at[0], pair_recv.at[p, group(o)], partner).start()

    ready = set()

    def pair_sum(p, o, h):
        if (p, group(o)) not in ready:
            ready.add((p, group(o)))
            wait_bytes(pair_in.at[p, 0 : 1 if o in (4, 0) else 2], pair_recv.at[p, group(o)])
        mine = own[p][rows_of(chip_at(o), c), half_cols(h)]
        return mine.astype(f32) + pair_in[p, o % chips, :, half_cols(h)].astype(f32)

    def rs_index(d, k, h):
        return 0 if k == 0 else 2 * k - 1 + (h != d)

    def rs_copy(p, d, k, h):
        i = rs_index(d, k, h)
        return rdma(send_buf.at[p, d, i], recv_buf.at[p, d, i], rs_send.at[0], rs_recv.at[p, d, i], neighbour(d))

    def rs_step(p, k, long_half):
        for d in range(2):
            h = d if long_half else 1 - d
            value = pair_sum(p, (4 - k if d == 0 else k - 4) if k else 4, h)
            if k >= 2 or (k == 1 and long_half):
                rs_copy(p, d, k - 1, h).wait_recv()
                value = value + recv_buf[p, d, rs_index(d, k - 1, h)].astype(f32)
            send_buf[p, d, rs_index(d, k, h)] = value.astype(bf16)
            rs_copy(p, d, k, h).start()

    def size_copy(p, e):
        return rdma(
            sizes.at[p],
            sizes_in.at[p, e - 1],
            size_send.at[0],
            size_recv.at[p],
            {"model": lax.rem(model + e, models)},
        )

    def finish_sum(p):
        total = jnp.zeros((share, 1), f32)
        for h in range(2):
            for d in range(2):
                rs_copy(p, d, 3, h).wait_recv()
            value = pair_sum(p, 0, h)
            for d in range(2):
                value = value + recv_buf[p, d, rs_index(d, 3, h)].astype(f32)
            value = value * rate
            mean[p, :, half_cols(h)] = value
            total = total + jnp.sum(value * value, axis=1, keepdims=True)
        param_loads[p].wait()
        weights = jnp.sum(param[p] * param[p], axis=1, keepdims=True)
        lane = lax.broadcasted_iota(jnp.int32, (share, 128), 1)
        sizes[p] = jnp.where(lane < 64, total, weights)
        for e in range(1, models):
            size_copy(p, e).start()

    def update(p):
        both = sizes[p]
        wait_bytes(sizes_in.at[p], size_recv.at[p])
        for e in range(1, models):
            both = both + sizes_in[p, e - 1]
        ratio = jnp.sqrt(both[:, 64:65]) * lax.rsqrt(both[:, 0:1] + eps)
        value = param[p] - learn_rate * (mean[p] * ratio)
        out = next_up if p == UP else next_down
        out[...] = value
        full[p][rows_of(z, c), :] = value.astype(bf16)
        at = full[p].at[rows_of(z, c), :]
        rdma(at, at, fwd_send.at[0], fwd_recv.at[forward_group(p, 0)], partner).start()

    def forward_group(p, k):
        return 0 if p == UP else k + 1

    def ag_index(d, k, h):
        return 2 * k + (h != d)

    def ag_copy(p, d, k, h, hop):
        chip = chip_at((-k - hop) if d == 0 else (k + hop))
        at = full[p].at[rows_of(chip, c), half_cols(h)]
        i = ag_index(d, k, h)
        return rdma(at, at, ag_send.at[0], ag_recv.at[p, d, i], neighbour(d))

    def forward(p, d, k, h):
        chip = chip_at((-k - 1) if d == 0 else (k + 1))
        at = full[p].at[rows_of(chip, c), half_cols(h)]
        rdma(at, at, fwd_send.at[0], fwd_recv.at[forward_group(p, k)], partner).start()

    def ag_arrive(p, k, long_half):
        for d in range(2):
            h = d if long_half else 1 - d
            ag_copy(p, d, k, h, 1).wait_recv()
            forward(p, d, k, h)

    def ag_step(p, k, long_half):
        for d in range(2):
            h = d if long_half else 1 - d
            if k:
                ag_copy(p, d, k - 1, h, 1).wait_recv()
                forward(p, d, k - 1, h)
            ag_copy(p, d, k, h, 0).start()

    def forwarded(p, k=0):
        count = chips if p == UP else (3, 2, 2, 1)[k]
        wait_bytes(pair_in.at[0, 0:count], fwd_recv.at[forward_group(p, k)])

    def row_copy(d, k, hop):
        chip = chip_at((-k - hop) if d == 0 else (k + hop))
        at = rows.at[c, chip]
        return rdma(at, at, row_send.at[0], row_recv.at[d, k], neighbour(d))

    def row_step(k):
        for d in range(2):
            if k:
                if d == 1 and k == 4:
                    continue
                row_copy(d, k - 1, 1).wait_recv()
            if k < 4 - d:
                row_copy(d, k, 0).start()

    def row_pair(core):
        return rdma(rows.at[core], rows.at[core], row_send.at[1], row_recv.at[0, 4], partner)

    def finish_rows():
        row_pair(1 - c).wait_recv()
        total = jnp.zeros((1, size), f32)
        gains = jnp.zeros((8, size), f32)
        wide = lax.broadcasted_iota(jnp.int32, (8, size), 1)
        for chip in range(chips):
            for core in range(2):
                total = total + rows[core, chip, :, :size]
                piece = jnp.broadcast_to(rows[core, chip, :, size:], (8, 128))
                piece = jnp.concatenate([piece] + [jnp.zeros((8, 128), f32)] * (size // 128 - 1), axis=1)
                start = (chip * 2 + core) * share
                moved = pltpu.roll(piece, start, 1) if start else piece
                gains = jnp.where((wide >= start) & (wide < start + share), moved, gains)
        gains = gains - learn_rate * (jnp.broadcast_to(total, (8, size)) * rate)
        half_norm[...] = gains[0].astype(bf16)
        shift = lax.rem(size - replica * share, size)
        next_norm[...] = pltpu.roll(gains, shift, 1)[0:1, 0:share]

    def turn_in(lo, hi):
        @pl.loop(lo, hi)
        def _(i):
            at = pl.ds(pl.multiple_of(i * 128, 128), 128)
            own_down[at, :] = raw_down[:, at].T

    low = (5 * chip_at(4)) // 4

    def turn_out(lo, hi):
        @pl.loop(lo, hi)
        def _(i):
            j = lax.rem(low + i, size // 128)
            at = pl.ds(pl.multiple_of(j * 128, 128), 128)
            half_down[:, at] = gathered[at, :].T

    L, S = True, False
    start_pairs(UP, 4)
    rs_step(UP, 0, L)
    start_pairs(UP, 3, -3)
    down_load.wait()
    turn_in(0, size // 128)
    rs_step(UP, 1, S)
    start_pairs(DOWN, 4, 3, -3)
    for load in row_loads:
        load.wait()
    rows[c, z, :, size:] = jnp.zeros((1, 128), jnp.float32)
    rows[c, z, :, :size] = norm_in[...].astype(jnp.float32)
    rows[c, z, :, size : size + share] = gain_in[...]
    rs_step(DOWN, 0, L)
    rs_step(DOWN, 1, S)
    start_pairs(UP, 2, -2)
    start_pairs(DOWN, 2, -2)
    rs_step(UP, 1, L)
    start_pairs(UP, 1, -1)
    start_pairs(DOWN, 1, -1)
    start_pairs(UP, 0)
    start_pairs(DOWN, 0)
    row_step(0)
    rs_step(UP, 2, S)
    rs_step(UP, 2, L)
    rs_step(DOWN, 1, L)
    rs_step(UP, 3, S)
    row_step(1)
    rs_step(UP, 3, L)
    rs_step(DOWN, 2, S)
    rs_step(DOWN, 2, L)
    row_step(2)
    finish_sum(UP)
    rs_step(DOWN, 3, S)
    update(UP)
    ag_step(UP, 0, L)
    rs_step(DOWN, 3, L)
    row_step(3)
    ag_step(UP, 0, S)
    ag_step(UP, 1, L)
    finish_sum(DOWN)
    ag_step(UP, 1, S)
    row_step(4)
    row_pair(c).start()
    update(DOWN)
    ag_step(DOWN, 0, L)
    ag_step(DOWN, 0, S)
    ag_step(UP, 2, L)
    ag_step(DOWN, 1, L)
    ag_step(DOWN, 1, S)
    finish_rows()
    ag_step(UP, 2, S)
    ag_step(DOWN, 2, L)
    ag_step(DOWN, 2, S)
    forwarded(DOWN, 0)
    turn_out(5, 7)
    ag_step(DOWN, 3, L)
    ag_step(UP, 3, L)
    forwarded(DOWN, 1)
    turn_out(4, 5)
    turn_out(7, 8)
    ag_arrive(UP, 2, S)
    ag_arrive(DOWN, 2, S)
    forwarded(DOWN, 2)
    turn_out(2, 4)
    turn_out(8, 10)
    ag_arrive(DOWN, 3, L)
    forwarded(DOWN, 3)
    turn_out(0, 2)
    ag_arrive(UP, 3, L)
    forwarded(UP)
    wait_bytes(pair_in, pair_send.at[0])
    wait_bytes(send_buf, rs_send.at[0])
    wait_bytes(send_buf, ag_send.at[0])
    wait_bytes(pair_in, fwd_send.at[0])
    wait_bytes(sizes_in, size_send.at[0])
    wait_bytes(rows.at[0, 0 : chips - 1], row_send.at[0])
    wait_bytes(rows.at[0], row_send.at[1])


def put(*refs):
    count = len(refs) // 2
    copies = [pltpu.make_async_copy(refs[i], refs[count + i], refs[-1].at[i]) for i in range(count)]
    for copy in copies:
        copy.start()
    for copy in copies:
        copy.wait()


def shards(chips, models, slope_up, slope_down, slope_norm, param_up, param_down, param_norm):
    size = slope_up.shape[-1]
    share = param_up.shape[0]
    f32, bf16 = jnp.float32, jnp.bfloat16
    hbm = pl.BlockSpec(memory_space=pltpu.HBM)
    vmem = pl.BlockSpec(memory_space=pltpu.VMEM)
    dma = pltpu.SemaphoreType.DMA
    results = (
        jax.ShapeDtypeStruct((size, size), bf16),
        jax.ShapeDtypeStruct((size, size), bf16),
        jax.ShapeDtypeStruct((share, size), f32),
        jax.ShapeDtypeStruct((share, size), f32),
        jax.ShapeDtypeStruct((size,), bf16),
        jax.ShapeDtypeStruct((1, share), f32),
    )
    arrays = (slope_up[0], slope_down[0], slope_norm, param_up, param_down.T, param_norm[None])
    made = pl.pallas_call(
        functools.partial(kernel, size, chips, models),
        name="summed_step",
        out_shape=tuple(pltpu.VMEM(r.shape, r.dtype) for r in results),
        in_specs=[hbm] * 6,
        out_specs=[vmem] * 6,
        scratch_shapes=[
            pltpu.VMEM((size, size), bf16),
            pltpu.VMEM((size, size), bf16),
            pltpu.VMEM((size, size), bf16),
            pltpu.VMEM((2, chips, share, size), bf16),
            pltpu.VMEM((2, 2, 7, share, size // 2), bf16),
            pltpu.VMEM((2, 2, 7, share, size // 2), bf16),
            pltpu.VMEM((size, size), bf16),
            pltpu.VMEM((2, share, size), f32),
            pltpu.VMEM((2, share, size), f32),
            pltpu.VMEM((2, share, 128), f32),
            pltpu.VMEM((2, models - 1, share, 128), f32),
            pltpu.VMEM((2, chips, 1, size + 128), f32),
            pltpu.VMEM((1, size), bf16),
            pltpu.VMEM((1, share), f32),
            dma((9,)),
            dma((1,)),
            dma((2, 5)),
            dma((1,)),
            dma((2, 2, 7)),
            dma((1,)),
            dma((2, 2, 7)),
            dma((1,)),
            dma((5,)),
            dma((1,)),
            dma((2,)),
            dma((2,)),
            dma((2, 5)),
        ],
        compiler_params=pltpu.CompilerParams(
            collective_id=0, has_side_effects=True, vmem_limit_bytes=48 * 1024 * 1024
        ),
    )(*(pltpu.with_memory_space_constraint(a, pltpu.HBM) for a in arrays))
    half_up, half_down, next_up, next_down, half_norm, next_norm = pl.pallas_call(
        put,
        name="put",
        out_shape=results,
        in_specs=[vmem] * 6,
        out_specs=[hbm] * 6,
        scratch_shapes=[dma((6,))],
        compiler_params=pltpu.CompilerParams(vmem_limit_bytes=1024 * 1024),
    )(*made)
    return (half_up, half_down, half_norm, next_up, next_down.T, next_norm[0])


def solution(mesh):
    chips = mesh.shape["replica"] // 2
    models = mesh.shape["model"]
    return jax.shard_map(
        functools.partial(shards, chips, models),
        mesh=mesh,
        in_specs=(
            P(("copy", "replica"), None, "model"),
            P(("copy", "replica"), "model", None),
            P(("copy", "replica"), None),
            P(("copy", "replica"), "model"),
            P(("copy", "model"), "replica"),
            P(("copy", "replica")),
        ),
        out_specs=(
            P("copy", "model"),
            P(("copy", "model"), None),
            P("copy"),
            P(("copy", "replica"), "model"),
            P(("copy", "model"), "replica"),
            P(("copy", "replica")),
        ),
        check_vma=False,
    )
```

time: 99 us -> 81.3 us (0.82)
  local copies, waits for them, and re-layouts: 15.4 us -> 0 us
  other arithmetic: 1.32 us -> 0 us
    unnamed x20 -> x0, local copies, waits for them, and re-layouts: 14.2 us -> none
    pallas_call x1, Pallas kernels: 81.4 us -> 77.5 us  [shards(): pl.pallas_call(functools.partial(kernel, size, chips, models), name='summ...]
    pallas_call x0 -> x1, Pallas kernels: none -> 3.09 us  [shards(): pl.pallas_call(put, name='put', out_shape=results, in_specs=[vmem] * 6, o...]
where the time goes in v2:
time: 81.3 us; the launch traced here: 81.2 us
  Pallas kernels  80.6 us (99%)
    pallas_call x1, Pallas kernels, shards(): pl.pallas_call(functools.partial(kernel, size, chips, models), name='summ...  77.5 us
    pallas_call x1, Pallas kernels, shards(): pl.pallas_call(put, name='put', out_shape=results, in_specs=[vmem] * 6, o...  3.09 us

profile of v2, /device:TPU:1, one launch (start us, length us, event | category | flops | bytes accessed | tf_op | source)
XLA Modules:
  0.0 81.2 jit_solution(15645065061041061810)
XLA Ops:
  0.6 77.5 %summed_step.1 = (bf16[1280,1280]{1,0:T(8,128)(2,1)S(1)}, bf16[1280,1280]{1,0:T(8,128)(2,1)S(1)}, f32[80,1280]{1,0:T(8,128)S(1)}, f32[80,1280]{1,0:T(8,128)S(1)}...) custom-call(bf16[1280,1280]{1,0:T(8,128)(2,1)} %bitcast.6, bf16[1280,1280]{1,0:T(8,128)(2,1)} %bitcast.7, ...), custom_call_target="tpu_custom_call" | custom-call | tf_op jit(solution)/shard_map/summed_step/pallas_call | solution.py:389
  78.1 3.1 %put.1 = (bf16[1280,1280]{1,0:T(8,128)(2,1)}, bf16[1280,1280]{1,0:T(8,128)(2,1)}, f32[80,1280]{1,0:T(8,128)}, f32[80,1280]{1,0:T(8,128)}, bf16[1280]{0:T(1024)(128)(2,1)}, /*index=5*/f32[1,80]{1,0:T(1,128)}) custom-call(bf16[1280,1280]{1,0:T(8,128)(2,1)S(1)} %get-tuple-element.18.refs_0_, bf16[1280,1280]{1,0:T(8,128)(2,1)S(1)} %get-tuple-element.19.refs_1_, ...), custom_call_target="tpu_custom_call" | custom-call | tf_op jit(solution)/shard_map/put/pallas_call | solution.py:428

commit v3 on v2

--- a/solution.py
+++ b/solution.py
@@ -56,6 +56,7 @@
     size_recv,
     row_send,
     row_recv,
+    last_sem,
 ):
     f32, bf16 = jnp.float32, jnp.bfloat16
     share = size // (2 * chips)
@@ -99,34 +100,35 @@
     up_loads = {}
     for o in order:
         at = chip_rows(chip_at(o))
-        sem = load_sem.at[max(group(o) - 1, 0)]
+        sem = load_sem.at[group(o)]
         up_loads[o] = pltpu.make_async_copy(up_hbm.at[at, :], own_up.at[at, :], sem)
-    down_load = pltpu.make_async_copy(down_hbm, raw_down, load_sem.at[4])
+    down_load = pltpu.make_async_copy(down_hbm, raw_down, load_sem.at[5])
     param_loads = [
-        pltpu.make_async_copy(param_up_hbm, param.at[UP], load_sem.at[5]),
-        pltpu.make_async_copy(param_down_hbm, param.at[DOWN], load_sem.at[6]),
+        pltpu.make_async_copy(param_up_hbm, param.at[UP], load_sem.at[6]),
+        pltpu.make_async_copy(param_down_hbm, param.at[DOWN], load_sem.at[7]),
     ]
     row_loads = [
-        pltpu.make_async_copy(norm_hbm, norm_in, load_sem.at[7]),
-        pltpu.make_async_copy(gain_hbm, gain_in, load_sem.at[8]),
+        pltpu.make_async_copy(norm_hbm, norm_in, load_sem.at[8]),
+        pltpu.make_async_copy(gain_hbm, gain_in, load_sem.at[9]),
     ]
-    for o in order[:3]:
-        up_loads[o].start()
+    up_loads[4].start()
 
     barrier = pltpu.get_barrier_semaphore()
     others = [partner, neighbour(0), neighbour(1)]
     others += [{"model": lax.rem(model + d, models)} for d in range(1, models)]
     for device in others:
         pl.semaphore_signal(barrier, inc=1, device_id=device, device_id_type=MESH)
-    wait_bytes(own_up.at[0 : 6 * share, :], load_sem.at[0])
+    up_loads[3].start()
+    up_loads[-3].start()
+    up_loads[4].wait()
     for load in [down_load] + row_loads + [up_loads[o] for o in order[3:]] + param_loads:
         load.start()
     pl.semaphore_wait(barrier, len(others))
 
     def start_pairs(p, *offsets):
         for o in offsets:
-            if p == UP and o in (2, 1, 0):
-                wait_bytes(own_up.at[0 : (4 if o else 2) * share, :], load_sem.at[group(o) - 1])
+            if p == UP and o in (3, 2, 1, 0):
+                wait_bytes(own_up.at[0 : (4 if o else 2) * share, :], load_sem.at[group(o)])
             src = own[p].at[rows_of(chip_at(o), 1 - c), :]
             rdma(src, pair_in.at[p, o % chips], pair_send.at[0], pair_recv.at[p, group(o)], partner).start()
 
@@ -196,8 +198,8 @@
         at = full[p].at[rows_of(z, c), :]
         rdma(at, at, fwd_send.at[0], fwd_recv.at[forward_group(p, 0)], partner).start()
 
-    def forward_group(p, k):
-        return 0 if p == UP else k + 1
+    def forward_group(p, k, long_half=False):
+        return (5 if k == 2 and long_half else 0) if p == UP else k + 1
 
     def ag_index(d, k, h):
         return 2 * k + (h != d)
@@ -206,35 +208,63 @@
         chip = chip_at((-k - hop) if d == 0 else (k + hop))
         at = full[p].at[rows_of(chip, c), half_cols(h)]
         i = ag_index(d, k, h)
-        return rdma(at, at, ag_send.at[0], ag_recv.at[p, d, i], neighbour(d))
+        return rdma(at, at, ag_send.at[0], ag_recv.at[p, i], neighbour(d))
 
     def forward(p, d, k, h):
         chip = chip_at((-k - 1) if d == 0 else (k + 1))
         at = full[p].at[rows_of(chip, c), half_cols(h)]
-        rdma(at, at, fwd_send.at[0], fwd_recv.at[forward_group(p, k)], partner).start()
-
-    def ag_arrive(p, k, long_half):
+        rdma(at, at, fwd_send.at[0], fwd_recv.at[forward_group(p, k, h == d)], partner).start()
+
+    def ag_wait(p, k, long_half):
+        wait_bytes(send_buf.at[0, 0, 0:2], ag_recv.at[p, 2 * k + (not long_half)])
         for d in range(2):
-            h = d if long_half else 1 - d
-            ag_copy(p, d, k, h, 1).wait_recv()
-            forward(p, d, k, h)
+            forward(p, d, k, d if long_half else 1 - d)
 
     def ag_step(p, k, long_half):
+        if k:
+            ag_wait(p, k - 1, long_half)
         for d in range(2):
-            h = d if long_half else 1 - d
-            if k:
-                ag_copy(p, d, k - 1, h, 1).wait_recv()
-                forward(p, d, k - 1, h)
-            ag_copy(p, d, k, h, 0).start()
+            ag_copy(p, d, k, d if long_half else 1 - d, 0).start()
 
     def forwarded(p, k=0):
-        count = chips if p == UP else (3, 2, 2, 1)[k]
+        count = chips - 2 if p == UP else (3, 2, 2, 1)[k]
         wait_bytes(pair_in.at[0, 0:count], fwd_recv.at[forward_group(p, k)])
+
+    def last_rows(d, hop):
+        chip = chip_at((-3 - hop) if d == 0 else (3 + hop))
+        return full[UP].at[chip_rows(chip), half_cols(d)]
+
+    def last_send():
+        @pl.when(c == 1)
+        def _():
+            wait_bytes(pair_in.at[0, 0:1], fwd_recv.at[5])
+            for d in range(2):
+                at = last_rows(d, 0)
+                rdma(at, at, last_sem.at[0], last_sem.at[1], neighbour(d)).start()
+
+    def last_wait():
+        @pl.when(c == 1)
+        def _():
+            wait_bytes(pair_in.at[0, 0:2], last_sem.at[1])
+            for d in range(2):
+                at = last_rows(d, 1)
+                rdma(at, at, last_sem.at[2], last_sem.at[3], partner).start()
+
+    def last_done():
+        @pl.when(c == 1)
+        def _():
+            wait_bytes(pair_in.at[0, 0:2], last_sem.at[0])
+            wait_bytes(pair_in.at[0, 0:2], last_sem.at[2])
+
+        @pl.when(c == 0)
+        def _():
+            wait_bytes(pair_in.at[0, 0:1], fwd_recv.at[5])
+            wait_bytes(pair_in.at[0, 0:2], last_sem.at[3])
 
     def row_copy(d, k, hop):
         chip = chip_at((-k - hop) if d == 0 else (k + hop))
         at = rows.at[c, chip]
-        return rdma(at, at, row_send.at[0], row_recv.at[d, k], neighbour(d))
+        return rdma(at, at, row_send.at[0], row_recv.at[d * 4 + k], neighbour(d))
 
     def row_step(k):
         for d in range(2):
@@ -246,7 +276,7 @@
                 row_copy(d, k, 0).start()
 
     def row_pair(core):
-        return rdma(rows.at[core], rows.at[core], row_send.at[1], row_recv.at[0, 4], partner)
+        return rdma(rows.at[core], rows.at[core], row_send.at[1], row_recv.at[7], partner)
 
     def finish_rows():
         row_pair(1 - c).wait_recv()
@@ -333,29 +363,31 @@
     ag_step(DOWN, 1, S)
     finish_rows()
     ag_step(UP, 2, S)
+    ag_wait(UP, 2, L)
     ag_step(DOWN, 2, L)
     ag_step(DOWN, 2, S)
     forwarded(DOWN, 0)
     turn_out(5, 7)
     ag_step(DOWN, 3, L)
-    ag_step(UP, 3, L)
+    last_send()
+    ag_wait(UP, 2, S)
     forwarded(DOWN, 1)
     turn_out(4, 5)
     turn_out(7, 8)
-    ag_arrive(UP, 2, S)
-    ag_arrive(DOWN, 2, S)
+    ag_wait(DOWN, 2, S)
     forwarded(DOWN, 2)
     turn_out(2, 4)
     turn_out(8, 10)
-    ag_arrive(DOWN, 3, L)
+    ag_wait(DOWN, 3, L)
+    last_wait()
     forwarded(DOWN, 3)
     turn_out(0, 2)
-    ag_arrive(UP, 3, L)
     forwarded(UP)
+    last_done()
     wait_bytes(pair_in, pair_send.at[0])
     wait_bytes(send_buf, rs_send.at[0])
-    wait_bytes(send_buf, ag_send.at[0])
-    wait_bytes(pair_in, fwd_send.at[0])
+    wait_bytes(own_up.at[0 : 13 * share, :], ag_send.at[0])
+    wait_bytes(own_up.at[0 : 15 * share, :], fwd_send.at[0])
     wait_bytes(sizes_in, size_send.at[0])
     wait_bytes(rows.at[0, 0 : chips - 1], row_send.at[0])
     wait_bytes(rows.at[0], row_send.at[1])
@@ -407,19 +439,20 @@
             pltpu.VMEM((2, chips, 1, size + 128), f32),
             pltpu.VMEM((1, size), bf16),
             pltpu.VMEM((1, share), f32),
-            dma((9,)),
+            dma((10,)),
             dma((1,)),
             dma((2, 5)),
             dma((1,)),
             dma((2, 2, 7)),
             dma((1,)),
-            dma((2, 2, 7)),
+            dma((2, 7)),
             dma((1,)),
-            dma((5,)),
+            dma((6,)),
             dma((1,)),
             dma((2,)),
             dma((2,)),
-            dma((2, 5)),
+            dma((8,)),
+            dma((4,)),
         ],
         compiler_params=pltpu.CompilerParams(
             collective_id=0, has_side_effects=True, vmem_limit_bytes=48 * 1024 * 1024

time: 81.3 us -> 80.7 us (level)
  no operation moved by 1% of the time
where the time goes in v3:
time: 80.7 us; the launch traced here: 80.6 us
  Pallas kernels  79.9 us (99%)
    pallas_call x1, Pallas kernels, shards(): pl.pallas_call(functools.partial(kernel, size, chips, models), name='summ...  76.9 us
    pallas_call x1, Pallas kernels, shards(): pl.pallas_call(put, name='put', out_shape=results, in_specs=[vmem] * 6, o...  3.09 us

profile of v3, /device:TPU:1, one launch (start us, length us, event | category | flops | bytes accessed | tf_op | source)
XLA Modules:
  0.0 80.6 jit_solution(832425954764270503)
XLA Ops:
  0.6 76.9 %summed_step.1 = (bf16[1280,1280]{1,0:T(8,128)(2,1)S(1)}, bf16[1280,1280]{1,0:T(8,128)(2,1)S(1)}, f32[80,1280]{1,0:T(8,128)S(1)}, f32[80,1280]{1,0:T(8,128)S(1)}...) custom-call(bf16[1280,1280]{1,0:T(8,128)(2,1)} %bitcast.6, bf16[1280,1280]{1,0:T(8,128)(2,1)} %bitcast.7, ...), custom_call_target="tpu_custom_call" | custom-call | tf_op jit(solution)/shard_map/summed_step/pallas_call | solution.py:421
  77.5 3.1 %put.1 = (bf16[1280,1280]{1,0:T(8,128)(2,1)}, bf16[1280,1280]{1,0:T(8,128)(2,1)}, f32[80,1280]{1,0:T(8,128)}, f32[80,1280]{1,0:T(8,128)}, bf16[1280]{0:T(1024)(128)(2,1)}, /*index=5*/f32[1,80]{1,0:T(1,128)}) custom-call(bf16[1280,1280]{1,0:T(8,128)(2,1)S(1)} %get-tuple-element.18.refs_0_, bf16[1280,1280]{1,0:T(8,128)(2,1)S(1)} %get-tuple-element.19.refs_1_, ...), custom_call_target="tpu_custom_call" | custom-call | tf_op jit(solution)/shard_map/put/pallas_call | solution.py:461

commit v4 on v3

--- a/solution.py
+++ b/solution.py
@@ -111,7 +111,8 @@
         pltpu.make_async_copy(norm_hbm, norm_in, load_sem.at[8]),
         pltpu.make_async_copy(gain_hbm, gain_in, load_sem.at[9]),
     ]
-    up_loads[4].start()
+    for load in [up_loads[4]] + row_loads:
+        load.start()
 
     barrier = pltpu.get_barrier_semaphore()
     others = [partner, neighbour(0), neighbour(1)]
@@ -121,7 +122,7 @@
     up_loads[3].start()
     up_loads[-3].start()
     up_loads[4].wait()
-    for load in [down_load] + row_loads + [up_loads[o] for o in order[3:]] + param_loads:
+    for load in [down_load] + [up_loads[o] for o in order[3:]] + param_loads:
         load.start()
     pl.semaphore_wait(barrier, len(others))
 
@@ -208,23 +209,27 @@
         chip = chip_at((-k - hop) if d == 0 else (k + hop))
         at = full[p].at[rows_of(chip, c), half_cols(h)]
         i = ag_index(d, k, h)
-        return rdma(at, at, ag_send.at[0], ag_recv.at[p, i], neighbour(d))
+        return rdma(at, at, ag_send.at[0], ag_recv.at[p, d, i], neighbour(d))
 
     def forward(p, d, k, h):
         chip = chip_at((-k - 1) if d == 0 else (k + 1))
         at = full[p].at[rows_of(chip, c), half_cols(h)]
         rdma(at, at, fwd_send.at[0], fwd_recv.at[forward_group(p, k, h == d)], partner).start()
 
-    def ag_wait(p, k, long_half):
-        wait_bytes(send_buf.at[0, 0, 0:2], ag_recv.at[p, 2 * k + (not long_half)])
+    def ag_wait(p, k, long_half, onward=False):
         for d in range(2):
-            forward(p, d, k, d if long_half else 1 - d)
+            h = d if long_half else 1 - d
+            ag_copy(p, d, k, h, 1).wait_recv()
+            forward(p, d, k, h)
+            if onward:
+                ag_copy(p, d, k + 1, h, 0).start()
 
     def ag_step(p, k, long_half):
         if k:
-            ag_wait(p, k - 1, long_half)
-        for d in range(2):
-            ag_copy(p, d, k, d if long_half else 1 - d, 0).start()
+            ag_wait(p, k - 1, long_half, True)
+        else:
+            for d in range(2):
+                ag_copy(p, d, k, d if long_half else 1 - d, 0).start()
 
     def forwarded(p, k=0):
         count = chips - 2 if p == UP else (3, 2, 2, 1)[k]
@@ -313,17 +318,18 @@
 
     L, S = True, False
     start_pairs(UP, 4)
+    for load in row_loads:
+        load.wait()
+    rows[c, z, :, size:] = jnp.zeros((1, 128), jnp.float32)
+    rows[c, z, :, :size] = norm_in[...].astype(jnp.float32)
+    rows[c, z, :, size : size + share] = gain_in[...]
+    row_step(0)
     rs_step(UP, 0, L)
     start_pairs(UP, 3, -3)
     down_load.wait()
     turn_in(0, size // 128)
     rs_step(UP, 1, S)
     start_pairs(DOWN, 4, 3, -3)
-    for load in row_loads:
-        load.wait()
-    rows[c, z, :, size:] = jnp.zeros((1, 128), jnp.float32)
-    rows[c, z, :, :size] = norm_in[...].astype(jnp.float32)
-    rows[c, z, :, size : size + share] = gain_in[...]
     rs_step(DOWN, 0, L)
     rs_step(DOWN, 1, S)
     start_pairs(UP, 2, -2)
@@ -333,7 +339,6 @@
     start_pairs(DOWN, 1, -1)
     start_pairs(UP, 0)
     start_pairs(DOWN, 0)
-    row_step(0)
     rs_step(UP, 2, S)
     rs_step(UP, 2, L)
     rs_step(DOWN, 1, L)
@@ -369,11 +374,11 @@
     forwarded(DOWN, 0)
     turn_out(5, 7)
     ag_step(DOWN, 3, L)
-    last_send()
     ag_wait(UP, 2, S)
     forwarded(DOWN, 1)
     turn_out(4, 5)
     turn_out(7, 8)
+    last_send()
     ag_wait(DOWN, 2, S)
     forwarded(DOWN, 2)
     turn_out(2, 4)
@@ -445,7 +450,7 @@
             dma((1,)),
             dma((2, 2, 7)),
             dma((1,)),
-            dma((2, 7)),
+            dma((2, 2, 7)),
             dma((1,)),
             dma((6,)),
             dma((1,)),

time: 80.7 us -> 80.5 us (level)
  no operation moved by 1% of the time
where the time goes in v4:
time: 80.5 us; the launch traced here: 80.4 us
  Pallas kernels  79.7 us (99%)
    pallas_call x1, Pallas kernels, shards(): pl.pallas_call(functools.partial(kernel, size, chips, models), name='summ...  76.6 us
    pallas_call x1, Pallas kernels, shards(): pl.pallas_call(put, name='put', out_shape=results, in_specs=[vmem] * 6, o...  3.09 us

profile of v4, /device:TPU:1, one launch (start us, length us, event | category | flops | bytes accessed | tf_op | source)
XLA Modules:
  0.0 80.4 jit_solution(2731780382485783972)
XLA Ops:
  0.6 76.6 %summed_step.1 = (bf16[1280,1280]{1,0:T(8,128)(2,1)S(1)}, bf16[1280,1280]{1,0:T(8,128)(2,1)S(1)}, f32[80,1280]{1,0:T(8,128)S(1)}, f32[80,1280]{1,0:T(8,128)S(1)}...) custom-call(bf16[1280,1280]{1,0:T(8,128)(2,1)} %bitcast.6, bf16[1280,1280]{1,0:T(8,128)(2,1)} %bitcast.7, ...), custom_call_target="tpu_custom_call" | custom-call | tf_op jit(solution)/shard_map/summed_step/pallas_call | solution.py:426
  77.3 3.1 %put.1 = (bf16[1280,1280]{1,0:T(8,128)(2,1)}, bf16[1280,1280]{1,0:T(8,128)(2,1)}, f32[80,1280]{1,0:T(8,128)}, f32[80,1280]{1,0:T(8,128)}, bf16[1280]{0:T(1024)(128)(2,1)}, /*index=5*/f32[1,80]{1,0:T(1,128)}) custom-call(bf16[1280,1280]{1,0:T(8,128)(2,1)S(1)} %get-tuple-element.18.refs_0_, bf16[1280,1280]{1,0:T(8,128)(2,1)S(1)} %get-tuple-element.19.refs_1_, ...), custom_call_target="tpu_custom_call" | custom-call | tf_op jit(solution)/shard_map/put/pallas_call | solution.py:466

commit v5 on v4

--- a/solution.py
+++ b/solution.py
@@ -136,7 +136,9 @@
     ready = set()
 
     def pair_sum(p, o, h):
-        if (p, group(o)) not in ready:
+        if (p, o) == (UP, 4):
+            wait_bytes(send_buf.at[0, 0, 0], pair_recv.at[UP, h * 5])
+        elif (p, group(o)) not in ready:
             ready.add((p, group(o)))
             wait_bytes(pair_in.at[p, 0 : 1 if o in (4, 0) else 2], pair_recv.at[p, group(o)])
         mine = own[p][rows_of(chip_at(o), c), half_cols(h)]
@@ -317,7 +319,9 @@
             half_down[:, at] = gathered[at, :].T
 
     L, S = True, False
-    start_pairs(UP, 4)
+    for h in range(2):
+        first = own_up.at[rows_of(chip_at(4), 1 - c), half_cols(h)]
+        rdma(first, pair_in.at[UP, 4, :, half_cols(h)], pair_send.at[0], pair_recv.at[UP, h * 5], partner).start()
     for load in row_loads:
         load.wait()
     rows[c, z, :, size:] = jnp.zeros((1, 128), jnp.float32)
@@ -446,7 +450,7 @@
             pltpu.VMEM((1, share), f32),
             dma((10,)),
             dma((1,)),
-            dma((2, 5)),
+            dma((2, 6)),
             dma((1,)),
             dma((2, 2, 7)),
             dma((1,)),

time: 80.5 us -> 80.3 us (level)
  no operation moved by 1% of the time
where the time goes in v5:
time: 80.3 us; the launch traced here: 80.2 us
  Pallas kernels  79.6 us (99%)
    pallas_call x1, Pallas kernels, shards(): pl.pallas_call(functools.partial(kernel, size, chips, models), name='summ...  76.5 us
    pallas_call x1, Pallas kernels, shards(): pl.pallas_call(put, name='put', out_shape=results, in_specs=[vmem] * 6, o...  3.09 us

profile of v5, /device:TPU:1, one launch (start us, length us, event | category | flops | bytes accessed | tf_op | source)
XLA Modules:
  0.0 80.2 jit_solution(7404021038639585429)
XLA Ops:
  0.6 76.5 %summed_step.1 = (bf16[1280,1280]{1,0:T(8,128)(2,1)S(1)}, bf16[1280,1280]{1,0:T(8,128)(2,1)S(1)}, f32[80,1280]{1,0:T(8,128)S(1)}, f32[80,1280]{1,0:T(8,128)S(1)}...) custom-call(bf16[1280,1280]{1,0:T(8,128)(2,1)} %bitcast.6, bf16[1280,1280]{1,0:T(8,128)(2,1)} %bitcast.7, ...), custom_call_target="tpu_custom_call" | custom-call | tf_op jit(solution)/shard_map/summed_step/pallas_call | solution.py:430
  77.1 3.1 %put.1 = (bf16[1280,1280]{1,0:T(8,128)(2,1)}, bf16[1280,1280]{1,0:T(8,128)(2,1)}, f32[80,1280]{1,0:T(8,128)}, f32[80,1280]{1,0:T(8,128)}, bf16[1280]{0:T(1024)(128)(2,1)}, /*index=5*/f32[1,80]{1,0:T(1,128)}) custom-call(bf16[1280,1280]{1,0:T(8,128)(2,1)S(1)} %get-tuple-element.18.refs_0_, bf16[1280,1280]{1,0:T(8,128)(2,1)S(1)} %get-tuple-element.19.refs_1_, ...), custom_call_target="tpu_custom_call" | custom-call | tf_op jit(solution)/shard_map/put/pallas_call | solution.py:470
